TPU v7x, 32 devices: a whole 2x2x4 slice. The times are simulated.
32 devices in a mesh: first: 4 (over y, x), second: 8 (over z, core).
Axes of the slice: x: 2, y: 2, z: 4, core: 2. Of those that a mesh axis runs over, the one named last changes fastest.
Arguments:
- pair_state: bfloat16 [96, 96, 128], P('first', 'second'), may hold values from -6 to 6
- in_gain: float32 [128], replicated, may hold values from 0.25 to 1.75
- left_weight: bfloat16 [128, 128], replicated, may hold values from -0.5 to 0.5
- right_weight: bfloat16 [128, 128], replicated, may hold values from -0.5 to 0.5
- mid_gain: float32 [128], replicated, may hold values from 0.25 to 1.75
- out_weight: bfloat16 [128, 128], replicated, may hold values from -0.5 to 0.5
- out_gate: bfloat16 [128, 128], replicated, may hold values from -0.5 to 0.5
Outputs:
- triangle_out: bfloat16 [96, 96, 128], P('first', 'second')
All inputs are finite; a program needn't handle non-finite values.
Results may differ from a plain program's by a relative error of at most 0.015.
Values may be sent and summed in bfloat16 or wider, within the bound.
A program may use at most 64 MiB of HBM per device.

v0:
```python
import jax
import jax.numpy as jnp
from jax import lax
from jax.sharding import PartitionSpec as P


def unit_channels(values, channel_gain):
    centred = values - jnp.mean(values, axis=-1, keepdims=True)
    return (
        centred
        * lax.rsqrt(jnp.mean(centred * centred, axis=-1, keepdims=True) + 1e-05)
        * channel_gain
    )


def make_factors(pair_in, in_gain, left_weight, right_weight):
    ready = unit_channels(pair_in.astype(jnp.float32), in_gain).astype(jnp.bfloat16)
    ready = lax.optimization_barrier(ready)
    left = jnp.einsum("ijc,cd->ijd", ready, left_weight, preferred_element_type=jnp.float32)
    right = jnp.einsum("ijc,cd->ijd", ready, right_weight, preferred_element_type=jnp.float32)
    return (ready, left.astype(jnp.bfloat16), right.astype(jnp.bfloat16))


def finish_pair(mixed, ready, mid_gain, out_weight, out_gate):
    scaled = unit_channels(mixed.astype(jnp.float32), mid_gain).astype(jnp.bfloat16)
    scaled = lax.optimization_barrier(scaled)
    gate = jax.nn.sigmoid(
        jnp.einsum("ijc,cd->ijd", ready, out_gate, preferred_element_type=jnp.float32)
    )
    return (
        jnp.einsum("ijd,dc->ijc", scaled, out_weight, preferred_element_type=jnp.float32) * gate
    ).astype(jnp.bfloat16)


def per_device(pair_state, in_gain, left_weight, right_weight, mid_gain, out_weight, out_gate):
    ready, left, right = make_factors(pair_state, in_gain, left_weight, right_weight)
    count = pair_state.shape[1] * lax.axis_size("second")
    left_lines, right_lines = (
        lax.all_to_all(left, "second", split_axis=2, concat_axis=1, tiled=True),
        lax.all_to_all(right, "second", split_axis=2, concat_axis=1, tiled=True),
    )

    def meet(piece):
        return jnp.einsum("ikd,jkd->ijd", left_lines, piece, preferred_element_type=jnp.float32)

    strip = meet(lax.all_gather(right_lines, "first", axis=0, tiled=True))
    strip = (strip * count ** (-0.5)).astype(jnp.bfloat16)
    mixed = lax.all_to_all(strip, "second", split_axis=1, concat_axis=2, tiled=True)
    return finish_pair(mixed, ready, mid_gain, out_weight, out_gate)


def solution(mesh):
    in_specs = (P("first", "second", None), P(), P(), P(), P(), P(), P())
    out_specs = P("first", "second", None)
    return jax.shard_map(
        per_device, mesh=mesh, in_specs=in_specs, out_specs=out_specs, check_vma=False
    )
```

profile of v0, /device:TPU:0, one launch (start us, length us, event | category | flops | bytes accessed | tf_op | source)
XLA Modules:
  0.0 47.7 jit_solution(16947037172463757196)
XLA Ops:
  0.0 1.0 %convert_reduce_fusion = f32[24,12]{0,1:T(8,128)S(1)} fusion(bf16[24,12,128]{2,0,1:T(8,128)(2,1)} %param.7), kind=kLoop, calls=%fused_computation.16 | loop fusion | flops 73440 | bytes 74880 | tf_op jit(solution)/shard_map/reduce_sum | solution.py:8
  1.0 1.1 %fusion.11 = f32[24,12]{0,1:T(8,128)S(1)} fusion(bf16[24,12,128]{2,0,1:T(8,128)(2,1)} %param.7, f32[24,12]{0,1:T(8,128)S(1)} %broadcast_multiply_fusion.1), kind=kLoop, calls=%fused_computation.19 | loop fusion | flops 147168 | bytes 76032 | tf_op jit(solution)/shard_map/reduce_sum | solution.py:11
  2.1 1.0 %fusion.13 = bf16[24,12,128]{2,0,1:T(8,128)(2,1)S(1)} fusion(bf16[24,12,128]{2,0,1:T(8,128)(2,1)} %param.7, f32[128]{0:T(128)} %param.8, f32[24,12]{0,1:T(8,128)S(1)} %add_rsqrt_fusion.1, f32[24,12]{0,1:T(8,128)S(1)} %broadcast_multiply_fusion.1), kind=kLoop, calls=%fused_computation.21 | loop fusion | flops 184320 | bytes 150272 | tf_op jit(solution)/shard_map/convert_element_type | solution.py:17
  3.2 0.2 convolution_convert_fusion.1
  3.3 0.4 copy.18
  3.8 1.1 %reshape.39 = bf16[8,2,2304]{2,1,0:T(2,128)(2,1)} reshape(bf16[128,12,24]{2,1,0:T(8,128)(2,1)S(1)} %bitcast.52) | data formatting | bytes 147456
  4.9 6.4 %all-to-all-start = ((bf16[8,2,2304]{2,1,0:T(2,128)(2,1)}), bf16[8,2,2304]{2,1,0:T(2,128)(2,1)S(1)}, u32[]{:S(2)}, u32[]{:S(2)}) async-start(bf16[8,2,2304]{2,1,0:T(2,128)(2,1)} %reshape.39), calls=%async_computation | async-start | bytes 147456 | tf_op jit(solution)/shard_map/all_to_all | solution.py:40
  11.3 0.2 convolution_convert_fusion
  11.5 0.4 copy.22
  11.9 1.1 %reshape.41 = bf16[8,2,2304]{2,1,0:T(2,128)(2,1)} reshape(bf16[128,12,24]{2,1,0:T(8,128)(2,1)S(1)} %bitcast.53) | data formatting | bytes 147456
  13.1 4.2 %all-to-all-done = bf16[8,2,2304]{2,1,0:T(2,128)(2,1)S(1)} async-done(((bf16[8,2,2304]{2,1,0:T(2,128)(2,1)}), bf16[8,2,2304]{2,1,0:T(2,128)(2,1)S(1)}, u32[]{:S(2)}, u32[]{:S(2)}) %all-to-all-start) | async-done | bytes 73760 | tf_op jit(solution)/shard_map/all_to_all | solution.py:40
  17.3 3.4 %all-to-all-start.1 = ((bf16[8,2,2304]{2,1,0:T(2,128)(2,1)}), bf16[8,2,2304]{2,1,0:T(2,128)(2,1)S(1)}, u32[]{:S(2)}, u32[]{:S(2)}) async-start(bf16[8,2,2304]{2,1,0:T(2,128)(2,1)} %reshape.41), calls=%async_computation.1 | async-start | bytes 147456 | tf_op jit(solution)/shard_map/all_to_all | solution.py:39
  20.7 0.6 %reshape.40 = bf16[128,12,24]{2,1,0:T(8,128)(2,1)S(1)} reshape(bf16[8,2,2304]{2,1,0:T(2,128)(2,1)S(1)} %all-to-all-done) | data formatting | bytes 147456
  21.3 0.1 copy.20
  21.4 0.4 copy.21
  21.7 10.4 %all_gather.3 = bf16[96,96,16]{1,0,2:T(8,128)(2,1)S(1)} all-gather(bf16[24,96,16]{1,0,2:T(8,128)(2,1)S(1)} %copy.21), channel_id=1, replica_groups=mesh['first'=4,'second'=8] {'first'}, dimensions={0}, use_global_device_ids=true | all-gather | bytes 368640 | tf_op jit(solution)/shard_map/all_gather | solution.py:46
  32.2 0.6 %reshape.42 = bf16[128,12,24]{2,1,0:T(8,128)(2,1)S(1)} reshape(bf16[8,2,2304]{2,1,0:T(2,128)(2,1)S(1)} %all-to-all-done.1) | data formatting | bytes 147456
  32.8 0.1 copy.24
  32.9 0.4 fusion.6
  33.3 0.4 copy.26
  33.6 0.5 %reshape.43 = bf16[8,2,2304]{2,1,0:T(2,128)(2,1)S(1)} reshape(bf16[96,16,24]{2,1,0:T(8,128)(2,1)S(1)} %bitcast.56) | data formatting | bytes 147456
  34.1 10.4 %all_to_all.45 = bf16[8,2,2304]{2,1,0:T(2,128)(2,1)S(1)} all-to-all(bf16[8,2,2304]{2,1,0:T(2,128)(2,1)S(1)} %reshape.43), channel_id=1, replica_groups=mesh['first'=4,'second'=8] {'second'}, dimensions={0} | all-to-all | bytes 147456 | tf_op jit(solution)/shard_map/all_to_all | solution.py:48
  44.5 0.5 %reshape.44 = bf16[96,16,24]{2,1,0:T(8,128)(2,1)S(1)} reshape(bf16[8,2,2304]{2,1,0:T(2,128)(2,1)S(1)} %all_to_all.45) | data formatting | bytes 147456
  45.1 0.1 fusion.7
  45.2 0.1 convert_bitcast_fusion
  45.3 0.1 multiply_reduce_fusion
  45.4 0.5 copy.27
  45.9 0.3 reshape.32
  46.3 0.1 multiply_convert_fusion
  46.4 0.2 copy-done.2
  46.7 0.2 fusion.15
  46.8 0.8 %fusion.5 = bf16[24,12,128]{2,0,1:T(8,128)(2,1)} fusion(f32[24,12,128]{2,0,1:T(8,128)S(1)} %fusion.15, bf16[24,12,128]{2,0,1:T(8,128)(2,1)S(1)} %fusion.13, bf16[128,128]{1,0:T(8,128)(2,1)S(1)} %copy-done.4), kind=kOutput, calls=%fused_computation.7 | convolution fusion | flops 9621504 | bytes 327680 | tf_op jit(solution)/shard_map/ijc,cd->ijd/dot_general | solution.py:28
  (14 shorter events, 0.0 us)
Async XLA Ops:
  0.0 3.2 %copy-start = (bf16[128,128]{1,0:T(8,128)(2,1)S(1)}, bf16[128,128]{1,0:T(8,128)(2,1)}, u32[]{:S(2)}) copy-start(bf16[128,128]{1,0:T(8,128)(2,1)} %param.10) | copy-start | bytes 98308
  0.0 11.3 %copy-start.1 = (bf16[128,128]{1,0:T(8,128)(2,1)S(1)}, bf16[128,128]{1,0:T(8,128)(2,1)}, u32[]{:S(2)}) copy-start(bf16[128,128]{1,0:T(8,128)(2,1)} %param.9) | copy-start | bytes 98308
  4.9 12.4 %all-to-all-start = ((bf16[8,2,2304]{2,1,0:T(2,128)(2,1)}), bf16[8,2,2304]{2,1,0:T(2,128)(2,1)S(1)}, u32[]{:S(2)}, u32[]{:S(2)}) async-start(bf16[8,2,2304]{2,1,0:T(2,128)(2,1)} %reshape.39), calls=%async_computation | async-start | bytes 147456 | tf_op jit(solution)/shard_map/all_to_all | solution.py:40
  17.3 14.9 %all-to-all-start.1 = ((bf16[8,2,2304]{2,1,0:T(2,128)(2,1)}), bf16[8,2,2304]{2,1,0:T(2,128)(2,1)S(1)}, u32[]{:S(2)}, u32[]{:S(2)}) async-start(bf16[8,2,2304]{2,1,0:T(2,128)(2,1)} %reshape.41), calls=%async_computation.1 | async-start | bytes 147456 | tf_op jit(solution)/shard_map/all_to_all | solution.py:39
  45.4 0.8 %copy-start.3 = (f32[128]{0:T(128)S(1)}, f32[128]{0:T(128)}, u32[]{:S(2)}) copy-start(f32[128]{0:T(128)} %param.11) | copy-start | bytes 1540
  45.9 0.8 %copy-start.2 = (bf16[128,128]{1,0:T(8,128)(2,1)S(1)}, bf16[128,128]{1,0:T(8,128)(2,1)}, u32[]{:S(2)}) copy-start(bf16[128,128]{1,0:T(8,128)(2,1)} %param.12) | copy-start | bytes 98308
  45.9 0.9 %copy-start.4 = (bf16[128,128]{1,0:T(8,128)(2,1)S(1)}, bf16[128,128]{1,0:T(8,128)(2,1)}, u32[]{:S(2)}) copy-start(bf16[128,128]{1,0:T(8,128)(2,1)} %param.13) | copy-start | bytes 98308
where the time goes:
time: 48.2 us; the launch traced here: 47.7 us
  blocking collectives  20.9 us (43%)
  starting transfers between devices  9.74 us (20%)
  local copies, waits for them, and re-layouts  7.34 us (15%)
  waiting for transfers between devices  4.22 us (9%)
  other arithmetic  3.56 us (7%)
  matrix products  1.7 us (4%)
    all_gather x1, blocking collectives, per_device(): strip = meet(lax.all_gather(right_lines, 'first', axis=0, tiled=True))  10.4 us
    all_to_all x1, blocking collectives, per_device(): lax.all_to_all(strip, 'second', split_axis=1, concat_axis=2, tiled=True)  10.4 us
    all_to_all x1, starting transfers between devices, per_device(): lax.all_to_all(right, 'second', split_axis=2, concat_axis=1, tiled=True)  6.39 us
    unnamed x16, local copies, waits for them, and re-layouts  4.78 us
    all_to_all x1, waiting for transfers between devices, per_device(): lax.all_to_all(right, 'second', split_axis=2, concat_axis=1, tiled=True)  4.22 us
    all_to_all x1, starting transfers between devices, per_device(): lax.all_to_all(left, 'second', split_axis=2, concat_axis=1, tiled=True)  3.35 us
    reduce_sum x2, other arithmetic, unit_channels(): jnp.mean(centred * centred, axis=-1, keepdims=True) + 1e-05  1.22 us
    reduce_sum x2, other arithmetic, unit_channels(): centred = values - jnp.mean(values, axis=-1, keepdims=True)  1.09 us
  transfers between devices with their start and end apart: 2, of which 1 were waited for; matrix products, arithmetic and copies ran while one was open for 6% of the time, Pallas kernels for 0%

commit v1 on v0

--- a/solution.py
+++ b/solution.py
@@ -1,7 +1,16 @@
+import functools
+
 import jax
 import jax.numpy as jnp
 from jax import lax
+from jax.experimental import pallas as pl
+from jax.experimental.pallas import tpu as pltpu
 from jax.sharding import PartitionSpec as P
+
+MESH = pl.DeviceIdType.MESH
+F32 = jnp.float32
+BF16 = jnp.bfloat16
+CORES = 2
 
 
 def unit_channels(values, channel_gain):
@@ -13,6 +22,202 @@
     )
 
 
+def bit_xor(left, right, count):
+    total, bit = 0, 1
+    while bit < count:
+        total = total + (left // bit % 2 + right // bit % 2) % 2 * bit
+        bit *= 2
+    return total
+
+
+def triangle_kernel(
+    groups, count,
+    x_ref, in_gain, left_weight, right_weight, mid_gain, out_weight, out_gate, out_ref,
+    spread, left_send, left_recv, right_send, right_recv, right_rows, left_f, right_f,
+    part_send, part_recv, own_part, gate,
+    left_sems, right_send_sems, right_recv_sems, part_send_sems, part_recv_sems,
+):
+    rows, cols, width = x_ref.shape
+    pitch = spread.shape[0] // rows
+    half = rows // CORES
+    pairs = rows * cols
+    a = lax.axis_index("first")
+    b = lax.axis_index("second")
+    z, c = b // CORES, b % CORES
+    other = 1 - c
+
+    def core_at(first, layer, core):
+        return {"first": first, "second": layer * CORES + core}
+
+    barrier = pltpu.get_barrier_semaphore()
+    peers = [core_at(a, z, other)]
+    for s in range(1, groups):
+        peers += [core_at(bit_xor(a, s, groups), z, c), core_at(bit_xor(a, s, groups), z, other)]
+        peers.append(core_at(a, bit_xor(z, s, groups), c))
+    for peer in peers:
+        pl.semaphore_signal(barrier, inc=1, device_id=peer, device_id_type=MESH)
+
+    for i in range(rows):
+        spread[i * pitch : i * pitch + cols, :] = x_ref[i].astype(F32)
+    values = jnp.concatenate([spread[pl.ds(k, rows, stride=pitch), :] for k in range(cols)], axis=0)
+    ready = unit_channels(values, in_gain[...].reshape(1, width)).astype(BF16)
+
+    right_rows[...] = jnp.dot(ready, right_weight[...], preferred_element_type=F32)
+    for p in range(CORES):
+        for k in range(cols):
+            right_f[p, k * half : (k + 1) * half, :] = right_rows[
+                k * rows + p * half : k * rows + (p + 1) * half, :
+            ]
+    for p in range(CORES):
+        right_send[p] = right_f[p].astype(BF16)
+
+    pl.semaphore_wait(barrier, len(peers))
+
+    right_copies = {}
+    for s in range(groups):
+        for r in range(CORES):
+            if s == 0 and r == 0:
+                continue
+            core = c if r == 0 else other
+            copy = pltpu.make_async_remote_copy(
+                src_ref=right_send.at[core],
+                dst_ref=right_recv.at[s, r],
+                send_sem=right_send_sems.at[s, r],
+                recv_sem=right_recv_sems.at[s, r],
+                device_id=core_at(bit_xor(a, s, groups), z, core),
+                device_id_type=MESH,
+            )
+            copy.start()
+            right_copies[s, r] = copy
+
+    left = jnp.dot(ready, left_weight[...], preferred_element_type=F32).astype(BF16)
+    left_send[...] = left
+    left_f[0] = left.astype(F32)
+    left_copy = pltpu.make_async_remote_copy(
+        src_ref=left_send,
+        dst_ref=left_recv,
+        send_sem=left_sems.at[0],
+        recv_sem=left_sems.at[1],
+        device_id=core_at(a, z, other),
+        device_id_type=MESH,
+    )
+    left_copy.start()
+
+    gate[...] = jax.nn.sigmoid(jnp.dot(ready, out_gate[...], preferred_element_type=F32))
+
+    left_copy.wait_recv()
+    left_f[1] = left_recv[...].astype(F32)
+
+    part_copies = []
+    for s in range(groups):
+        if s == 0:
+            right_f[0] = right_send[c].astype(F32)
+        else:
+            right_copies[s, 0].wait_recv()
+            right_f[0] = right_recv[s, 0].astype(F32)
+        right_copies[s, 1].wait_recv()
+        right_f[1] = right_recv[s, 1].astype(F32)
+
+        def step(k, sums):
+            sums = list(sums)
+            for r in range(CORES):
+                line = left_f[r, pl.ds(pl.multiple_of(k * rows, 8), rows), :]
+                for j in range(half):
+                    sums[j] = sums[j] + line * right_f[r, pl.ds(k * half + j, 1), :]
+            return tuple(sums)
+
+        sums = lax.fori_loop(
+            0, cols, step, tuple(jnp.zeros((rows, width), F32) for _ in range(half))
+        )
+        part = jnp.concatenate(sums, axis=0)
+        part_send[s] = part.astype(BF16)
+        layer = bit_xor(a, s, groups)
+        turn = bit_xor(layer, z, groups)
+        copy = pltpu.make_async_remote_copy(
+            src_ref=part_send.at[s],
+            dst_ref=part_recv.at[turn],
+            send_sem=part_send_sems.at[s],
+            recv_sem=part_recv_sems.at[turn],
+            device_id=core_at(a, layer, c),
+            device_id_type=MESH,
+        )
+
+        @pl.when(turn != 0)
+        def _():
+            copy.start()
+
+        @pl.when(turn == 0)
+        def _():
+            own_part[...] = part
+
+        part_copies.append((turn, copy))
+
+    total = own_part[...]
+    for t in range(1, groups):
+        pltpu.make_async_remote_copy(
+            src_ref=part_send.at[0],
+            dst_ref=part_recv.at[t],
+            send_sem=part_send_sems.at[0],
+            recv_sem=part_recv_sems.at[t],
+            device_id=core_at(a, bit_xor(z, t, groups), c),
+            device_id_type=MESH,
+        ).wait_recv()
+        total = total + part_recv[t].astype(F32)
+
+    mixed = (total * count ** (-0.5)).astype(BF16).astype(F32)
+    scaled = unit_channels(mixed, mid_gain[...].reshape(1, width)).astype(BF16)
+    right_rows[...] = (
+        jnp.dot(scaled, out_weight[...], preferred_element_type=F32) * gate[...]
+    )
+    for i in range(rows):
+        out_ref[i] = right_rows[pl.ds(i, cols, stride=rows), :].astype(BF16)
+
+    left_copy.wait_send()
+    for copy in right_copies.values():
+        copy.wait_send()
+    for turn, copy in part_copies:
+
+        @pl.when(turn != 0)
+        def _(copy=copy):
+            copy.wait_send()
+
+
+def by_kernel(pair_state, in_gain, left_weight, right_weight, mid_gain, out_weight, out_gate):
+    rows, cols, width = pair_state.shape
+    groups = lax.axis_size("first")
+    count = cols * lax.axis_size("second")
+    pairs = rows * cols
+    half = pairs // CORES
+    pitch = -(-cols // 8) * 8
+    vmem = pl.BlockSpec(memory_space=pltpu.VMEM)
+    return pl.pallas_call(
+        functools.partial(triangle_kernel, groups, count),
+        out_shape=jax.ShapeDtypeStruct((rows, cols, width), BF16),
+        in_specs=[vmem] * 7,
+        out_specs=vmem,
+        scratch_shapes=[
+            pltpu.VMEM((rows * pitch, width), F32),
+            pltpu.VMEM((pairs, width), BF16),
+            pltpu.VMEM((pairs, width), BF16),
+            pltpu.VMEM((CORES, half, width), BF16),
+            pltpu.VMEM((groups, CORES, half, width), BF16),
+            pltpu.VMEM((pairs, width), F32),
+            pltpu.VMEM((CORES, pairs, width), F32),
+            pltpu.VMEM((CORES, half, width), F32),
+            pltpu.VMEM((groups, pairs, width), BF16),
+            pltpu.VMEM((groups, pairs, width), BF16),
+            pltpu.VMEM((pairs, width), F32),
+            pltpu.VMEM((pairs, width), F32),
+            pltpu.SemaphoreType.DMA((2,)),
+            pltpu.SemaphoreType.DMA((groups, CORES)),
+            pltpu.SemaphoreType.DMA((groups, CORES)),
+            pltpu.SemaphoreType.DMA((groups,)),
+            pltpu.SemaphoreType.DMA((groups,)),
+        ],
+        compiler_params=pltpu.CompilerParams(collective_id=0, has_side_effects=True),
+    )(pair_state, in_gain, left_weight, right_weight, mid_gain, out_weight, out_gate)
+
+
 def make_factors(pair_in, in_gain, left_weight, right_weight):
     ready = unit_channels(pair_in.astype(jnp.float32), in_gain).astype(jnp.bfloat16)
     ready = lax.optimization_barrier(ready)
@@ -32,7 +237,7 @@
     ).astype(jnp.bfloat16)
 
 
-def per_device(pair_state, in_gain, left_weight, right_weight, mid_gain, out_weight, out_gate):
+def by_collectives(pair_state, in_gain, left_weight, right_weight, mid_gain, out_weight, out_gate):
     ready, left, right = make_factors(pair_state, in_gain, left_weight, right_weight)
     count = pair_state.shape[1] * lax.axis_size("second")
     left_lines, right_lines = (
@@ -49,6 +254,20 @@
     return finish_pair(mixed, ready, mid_gain, out_weight, out_gate)
 
 
+def per_device(pair_state, *rest):
+    groups, parts = lax.axis_size("first"), lax.axis_size("second")
+    rows, cols, width = pair_state.shape
+    fits = (
+        parts == CORES * groups
+        and groups & (groups - 1) == 0
+        and rows == CORES * cols
+        and rows % 8 == 0
+        and rows * cols % 32 == 0
+        and rows // 8 * cols <= 48
+    )
+    return (by_kernel if fits else by_collectives)(pair_state, *rest)
+
+
 def solution(mesh):
     in_specs = (P("first", "second", None), P(), P(), P(), P(), P(), P())
     out_specs = P("first", "second", None)

time: 48.2 us -> 21.6 us (0.45)
  the two profiles are of different devices: /device:TPU:0 before, /device:TPU:6 now
where the time goes in v1:
time: 21.6 us; the launch traced here: 21.4 us
  Pallas kernels  18.4 us (85%)
  local copies, waits for them, and re-layouts  3.07 us (14%)
    pallas_call x1, Pallas kernels, by_kernel(): pl.pallas_call(functools.partial(triangle_kernel, groups, count), out_sha...  18.4 us
    pallas_call x1, local copies, waits for them, and re-layouts, by_kernel(): pl.pallas_call(functools.partial(triangle_kernel, groups, count), out_sha...  1.55 us
    unnamed x1, local copies, waits for them, and re-layouts  1.52 us

profile of v1, /device:TPU:6, one launch (start us, length us, event | category | flops | bytes accessed | tf_op | source)
XLA Modules:
  0.0 21.4 jit_solution(11209575237560319182)
XLA Ops:
  0.0 1.5 %copy.8.x_ref = bf16[24,12,128]{2,1,0:T(8,128)(2,1)} copy(bf16[24,12,128]{2,0,1:T(8,128)(2,1)} %param.7) | data formatting | bytes 147456 | tf_op args[0]
  1.5 18.4 %shard_map.73 = bf16[24,12,128]{2,1,0:T(8,128)(2,1)} custom-call(bf16[24,12,128]{2,1,0:T(8,128)(2,1)} %copy.8.x_ref, f32[128]{0:T(128)} %in_gain.1, bf16[128,128]{1,0:T(8,128)(2,1)} %left_weight.1, bf16[128,128]{1,0:T(8,128)(2,1)} %right_weight.1, f32[128]{0:T(128)} %mid_gain.1, bf16[128,128]{1,0:T(8,128)(2,1)} %out_weight.1, bf16[128,128]{1,0:T(8,128)(2,1)} %out_gate.1), custom_call_target="tpu_custom_call" | custom-call | tf_op jit(solution)/shard_map/pallas_call | solution.py:193
  19.9 1.5 %copy.9 = bf16[24,12,128]{2,0,1:T(8,128)(2,1)} copy(bf16[24,12,128]{2,1,0:T(8,128)(2,1)} %shard_map.73) | data formatting | bytes 147456 | tf_op jit(solution)/shard_map/pallas_call | solution.py:193

commit v2 on v1

--- a/solution.py
+++ b/solution.py
@@ -33,12 +33,11 @@
 def triangle_kernel(
     groups, count,
     x_ref, in_gain, left_weight, right_weight, mid_gain, out_weight, out_gate, out_ref,
-    spread, left_send, left_recv, right_send, right_recv, right_rows, left_f, right_f,
+    left_send, left_recv, right_send, right_recv, right_rows, left_f, right_f,
     part_send, part_recv, own_part, gate,
     left_sems, right_send_sems, right_recv_sems, part_send_sems, part_recv_sems,
 ):
-    rows, cols, width = x_ref.shape
-    pitch = spread.shape[0] // rows
+    cols, rows, width = x_ref.shape
     half = rows // CORES
     pairs = rows * cols
     a = lax.axis_index("first")
@@ -57,9 +56,7 @@
     for peer in peers:
         pl.semaphore_signal(barrier, inc=1, device_id=peer, device_id_type=MESH)
 
-    for i in range(rows):
-        spread[i * pitch : i * pitch + cols, :] = x_ref[i].astype(F32)
-    values = jnp.concatenate([spread[pl.ds(k, rows, stride=pitch), :] for k in range(cols)], axis=0)
+    values = x_ref[...].astype(F32).reshape(pairs, width)
     ready = unit_channels(values, in_gain[...].reshape(1, width)).astype(BF16)
 
     right_rows[...] = jnp.dot(ready, right_weight[...], preferred_element_type=F32)
@@ -166,11 +163,8 @@
 
     mixed = (total * count ** (-0.5)).astype(BF16).astype(F32)
     scaled = unit_channels(mixed, mid_gain[...].reshape(1, width)).astype(BF16)
-    right_rows[...] = (
-        jnp.dot(scaled, out_weight[...], preferred_element_type=F32) * gate[...]
-    )
-    for i in range(rows):
-        out_ref[i] = right_rows[pl.ds(i, cols, stride=rows), :].astype(BF16)
+    result = jnp.dot(scaled, out_weight[...], preferred_element_type=F32) * gate[...]
+    out_ref[...] = result.reshape(cols, rows, width).astype(BF16)
 
     left_copy.wait_send()
     for copy in right_copies.values():
@@ -188,15 +182,13 @@
     count = cols * lax.axis_size("second")
     pairs = rows * cols
     half = pairs // CORES
-    pitch = -(-cols // 8) * 8
     vmem = pl.BlockSpec(memory_space=pltpu.VMEM)
-    return pl.pallas_call(
+    changed = pl.pallas_call(
         functools.partial(triangle_kernel, groups, count),
-        out_shape=jax.ShapeDtypeStruct((rows, cols, width), BF16),
+        out_shape=jax.ShapeDtypeStruct((cols, rows, width), BF16),
         in_specs=[vmem] * 7,
         out_specs=vmem,
         scratch_shapes=[
-            pltpu.VMEM((rows * pitch, width), F32),
             pltpu.VMEM((pairs, width), BF16),
             pltpu.VMEM((pairs, width), BF16),
             pltpu.VMEM((CORES, half, width), BF16),
@@ -215,7 +207,11 @@
             pltpu.SemaphoreType.DMA((groups,)),
         ],
         compiler_params=pltpu.CompilerParams(collective_id=0, has_side_effects=True),
-    )(pair_state, in_gain, left_weight, right_weight, mid_gain, out_weight, out_gate)
+    )(
+        jnp.swapaxes(pair_state, 0, 1),
+        in_gain, left_weight, right_weight, mid_gain, out_weight, out_gate,
+    )
+    return jnp.swapaxes(changed, 0, 1)
 
 
 def make_factors(pair_in, in_gain, left_weight, right_weight):

time: 21.6 us -> 20 us (0.926)
  local copies, waits for them, and re-layouts: 3.07 us -> 1.52 us
    pallas_call x1 -> x0, local copies, waits for them, and re-layouts: 1.55 us -> none  [by_kernel(): pl.pallas_call(functools.partial(triangle_kernel, groups, count), out_sha...]
where the time goes in v2:
time: 20 us; the launch traced here: 19.8 us
  Pallas kernels  18.3 us (92%)
  local copies, waits for them, and re-layouts  1.52 us (8%)
    pallas_call x1, Pallas kernels, by_kernel(): pl.pallas_call(functools.partial(triangle_kernel, groups, count), out_sha...  18.3 us
    unnamed x1, local copies, waits for them, and re-layouts  1.52 us

profile of v2, /device:TPU:6, one launch (start us, length us, event | category | flops | bytes accessed | tf_op | source)
XLA Modules:
  0.0 19.8 jit_solution(9341240424742238187)
XLA Ops:
  0.0 18.3 %shard_map.73 = bf16[12,24,128]{2,1,0:T(8,128)(2,1)} custom-call(bf16[12,24,128]{2,1,0:T(8,128)(2,1)} %bitcast.3, f32[128]{0:T(128)} %in_gain.1, bf16[128,128]{1,0:T(8,128)(2,1)} %left_weight.1, bf16[128,128]{1,0:T(8,128)(2,1)} %right_weight.1, f32[128]{0:T(128)} %mid_gain.1, bf16[128,128]{1,0:T(8,128)(2,1)} %out_weight.1, bf16[128,128]{1,0:T(8,128)(2,1)} %out_gate.1), custom_call_target="tpu_custom_call" | custom-call | tf_op jit(solution)/shard_map/pallas_call | solution.py:186
  18.3 1.5 %copy.9 = bf16[24,12,128]{2,0,1:T(8,128)(2,1)} copy(bf16[24,12,128]{2,0,1:T(8,128)(2,1)} %bitcast.2) | data formatting | bytes 147456

commit v3 on v2

--- a/solution.py
+++ b/solution.py
@@ -32,7 +32,9 @@
 
 def triangle_kernel(
     groups, count,
-    x_ref, in_gain, left_weight, right_weight, mid_gain, out_weight, out_gate, out_ref,
+    x_hbm, in_gain_hbm, left_weight_hbm, right_weight_hbm, mid_gain_hbm, out_weight_hbm,
+    out_gate_hbm, out_ref,
+    x_ref, in_gain, left_weight, right_weight, mid_gain, out_weight, out_gate, fetch_sems,
     left_send, left_recv, right_send, right_recv, right_rows, left_f, right_f,
     part_send, part_recv, own_part, gate,
     left_sems, right_send_sems, right_recv_sems, part_send_sems, part_recv_sems,
@@ -56,6 +58,19 @@
     for peer in peers:
         pl.semaphore_signal(barrier, inc=1, device_id=peer, device_id_type=MESH)
 
+    fetches = [
+        pltpu.make_async_copy(src, dst, fetch_sems.at[n])
+        for n, (src, dst) in enumerate([
+            (x_hbm, x_ref), (in_gain_hbm, in_gain), (right_weight_hbm, right_weight),
+            (left_weight_hbm, left_weight), (out_gate_hbm, out_gate),
+            (mid_gain_hbm, mid_gain), (out_weight_hbm, out_weight),
+        ])
+    ]
+    for fetch in fetches:
+        fetch.start()
+    for fetch in fetches:
+        fetch.wait()
+
     values = x_ref[...].astype(F32).reshape(pairs, width)
     ready = unit_channels(values, in_gain[...].reshape(1, width)).astype(BF16)
 
@@ -70,22 +85,28 @@
 
     pl.semaphore_wait(barrier, len(peers))
 
-    right_copies = {}
-    for s in range(groups):
-        for r in range(CORES):
-            if s == 0 and r == 0:
-                continue
-            core = c if r == 0 else other
-            copy = pltpu.make_async_remote_copy(
-                src_ref=right_send.at[core],
-                dst_ref=right_recv.at[s, r],
-                send_sem=right_send_sems.at[s, r],
-                recv_sem=right_recv_sems.at[s, r],
-                device_id=core_at(bit_xor(a, s, groups), z, core),
-                device_id_type=MESH,
-            )
-            copy.start()
-            right_copies[s, r] = copy
+    inner = (a % (groups - 1) + groups - 2) // (groups - 1)
+    turns = [0] + [
+        inner * s + (1 - inner) * ((groups - 1) if s == 1 else s - 1)
+        for s in range(1, groups)
+    ]
+
+    def right_copy(s, r):
+        core = c if r == 0 else other
+        return pltpu.make_async_remote_copy(
+            src_ref=right_send.at[core],
+            dst_ref=right_recv.at[s, r],
+            send_sem=right_send_sems.at[s, r],
+            recv_sem=right_recv_sems.at[s, r],
+            device_id=core_at(bit_xor(a, s, groups), z, core),
+            device_id_type=MESH,
+        )
+
+    right_copies = [
+        right_copy(s, r) for n, s in enumerate(turns) for r in range(CORES) if (n, r) != (0, 0)
+    ]
+    for copy in right_copies:
+        copy.start()
 
     left = jnp.dot(ready, left_weight[...], preferred_element_type=F32).astype(BF16)
     left_send[...] = left
@@ -106,13 +127,13 @@
     left_f[1] = left_recv[...].astype(F32)
 
     part_copies = []
-    for s in range(groups):
-        if s == 0:
+    for n, s in enumerate(turns):
+        if n == 0:
             right_f[0] = right_send[c].astype(F32)
         else:
-            right_copies[s, 0].wait_recv()
+            right_copy(s, 0).wait_recv()
             right_f[0] = right_recv[s, 0].astype(F32)
-        right_copies[s, 1].wait_recv()
+        right_copy(s, 1).wait_recv()
         right_f[1] = right_recv[s, 1].astype(F32)
 
         def step(k, sums):
@@ -127,13 +148,13 @@
             0, cols, step, tuple(jnp.zeros((rows, width), F32) for _ in range(half))
         )
         part = jnp.concatenate(sums, axis=0)
-        part_send[s] = part.astype(BF16)
+        part_send[n] = part.astype(BF16)
         layer = bit_xor(a, s, groups)
         turn = bit_xor(layer, z, groups)
         copy = pltpu.make_async_remote_copy(
-            src_ref=part_send.at[s],
+            src_ref=part_send.at[n],
             dst_ref=part_recv.at[turn],
-            send_sem=part_send_sems.at[s],
+            send_sem=part_send_sems.at[n],
             recv_sem=part_recv_sems.at[turn],
             device_id=core_at(a, layer, c),
             device_id_type=MESH,
@@ -167,7 +188,7 @@
     out_ref[...] = result.reshape(cols, rows, width).astype(BF16)
 
     left_copy.wait_send()
-    for copy in right_copies.values():
+    for copy in right_copies:
         copy.wait_send()
     for turn, copy in part_copies:
 
@@ -182,13 +203,20 @@
     count = cols * lax.axis_size("second")
     pairs = rows * cols
     half = pairs // CORES
-    vmem = pl.BlockSpec(memory_space=pltpu.VMEM)
     changed = pl.pallas_call(
         functools.partial(triangle_kernel, groups, count),
         out_shape=jax.ShapeDtypeStruct((cols, rows, width), BF16),
-        in_specs=[vmem] * 7,
-        out_specs=vmem,
+        in_specs=[pl.BlockSpec(memory_space=pltpu.MemorySpace.HBM)] * 7,
+        out_specs=pl.BlockSpec(memory_space=pltpu.VMEM),
         scratch_shapes=[
+            pltpu.VMEM((cols, rows, width), BF16),
+            pltpu.VMEM((width,), F32),
+            pltpu.VMEM(left_weight.shape, BF16),
+            pltpu.VMEM(right_weight.shape, BF16),
+            pltpu.VMEM((width,), F32),
+            pltpu.VMEM(out_weight.shape, BF16),
+            pltpu.VMEM(out_gate.shape, BF16),
+            pltpu.SemaphoreType.DMA((7,)),
             pltpu.VMEM((pairs, width), BF16),
             pltpu.VMEM((pairs, width), BF16),
             pltpu.VMEM((CORES, half, width), BF16),
@@ -206,10 +234,17 @@
             pltpu.SemaphoreType.DMA((groups,)),
             pltpu.SemaphoreType.DMA((groups,)),
         ],
-        compiler_params=pltpu.CompilerParams(collective_id=0, has_side_effects=True),
+        compiler_params=pltpu.CompilerParams(
+            collective_id=0, has_side_effects=True, vmem_limit_bytes=8 * 1024 * 1024
+        ),
     )(
-        jnp.swapaxes(pair_state, 0, 1),
-        in_gain, left_weight, right_weight, mid_gain, out_weight, out_gate,
+        *(
+            pltpu.with_memory_space_constraint(value, pltpu.MemorySpace.HBM)
+            for value in (
+                jnp.swapaxes(pair_state, 0, 1),
+                in_gain, left_weight, right_weight, mid_gain, out_weight, out_gate,
+            )
+        )
     )
     return jnp.swapaxes(changed, 0, 1)
 
@@ -255,6 +290,7 @@
     rows, cols, width = pair_state.shape
     fits = (
         parts == CORES * groups
+        and groups > 1
         and groups & (groups - 1) == 0
         and rows == CORES * cols
         and rows % 8 == 0

time: 20 us -> 17.7 us (0.89)
  the two profiles are of different devices: /device:TPU:6 before, /device:TPU:13 now
where the time goes in v3:
time: 17.7 us; the launch traced here: 17.5 us
  Pallas kernels  16.9 us (95%)
  local copies, waits for them, and re-layouts  0.64 us (4%)
    pallas_call x1, Pallas kernels, by_kernel(): pl.pallas_call(functools.partial(triangle_kernel, groups, count), out_sha...  16.9 us
    unnamed x1, local copies, waits for them, and re-layouts  0.64 us

profile of v3, /device:TPU:13, one launch (start us, length us, event | category | flops | bytes accessed | tf_op | source)
XLA Modules:
  0.0 17.5 jit_solution(5179617461528968548)
XLA Ops:
  0.0 16.9 %shard_map.73 = bf16[12,24,128]{2,1,0:T(8,128)(2,1)S(1)} custom-call(bf16[12,24,128]{2,1,0:T(8,128)(2,1)} %bitcast.3, f32[128]{0:T(128)} %in_gain_hbm.1, bf16[128,128]{1,0:T(8,128)(2,1)} %left_weight_hbm.1, bf16[128,128]{1,0:T(8,128)(2,1)} %right_weight_hbm.1, f32[128]{0:T(128)} %mid_gain_hbm.1, bf16[128,128]{1,0:T(8,128)(2,1)} %out_weight_hbm.1, ...), custom_call_target="tpu_custom_call" | custom-call | tf_op jit(solution)/shard_map/pallas_call | solution.py:206
  16.9 0.6 %copy.9 = bf16[24,12,128]{2,0,1:T(8,128)(2,1)} copy(bf16[24,12,128]{2,0,1:T(8,128)(2,1)S(1)} %bitcast.2) | data formatting | bytes 147456

commit v4 on v3

--- a/solution.py
+++ b/solution.py
@@ -11,6 +11,7 @@
 F32 = jnp.float32
 BF16 = jnp.bfloat16
 CORES = 2
+PIECES = 2
 
 
 def unit_channels(values, channel_gain):
@@ -31,7 +32,7 @@
 
 
 def triangle_kernel(
-    groups, count,
+    groups, count, pieces,
     x_hbm, in_gain_hbm, left_weight_hbm, right_weight_hbm, mid_gain_hbm, out_weight_hbm,
     out_gate_hbm, out_ref,
     x_ref, in_gain, left_weight, right_weight, mid_gain, out_weight, out_gate, fetch_sems,
@@ -41,6 +42,7 @@
 ):
     cols, rows, width = x_ref.shape
     half = rows // CORES
+    some = half // pieces
     pairs = rows * cols
     a = lax.axis_index("first")
     b = lax.axis_index("second")
@@ -68,46 +70,48 @@
     ]
     for fetch in fetches:
         fetch.start()
-    for fetch in fetches:
-        fetch.wait()
-
+    got_x, got_in_gain, got_right, got_left, got_gate, got_mid_gain, got_out = fetches
+
+    got_x.wait()
+    got_in_gain.wait()
     values = x_ref[...].astype(F32).reshape(pairs, width)
     ready = unit_channels(values, in_gain[...].reshape(1, width)).astype(BF16)
 
+    got_right.wait()
     right_rows[...] = jnp.dot(ready, right_weight[...], preferred_element_type=F32)
     for p in range(CORES):
-        for k in range(cols):
-            right_f[p, k * half : (k + 1) * half, :] = right_rows[
-                k * rows + p * half : k * rows + (p + 1) * half, :
-            ]
-    for p in range(CORES):
-        right_send[p] = right_f[p].astype(BF16)
+        for h in range(pieces):
+            for k in range(cols):
+                start = k * rows + p * half + h * some
+                right_f[p, k * some : (k + 1) * some, :] = right_rows[start : start + some, :]
+            right_send[p, h] = right_f[p].astype(BF16)
 
     pl.semaphore_wait(barrier, len(peers))
 
-    inner = (a % (groups - 1) + groups - 2) // (groups - 1)
-    turns = [0] + [
-        inner * s + (1 - inner) * ((groups - 1) if s == 1 else s - 1)
-        for s in range(1, groups)
-    ]
-
-    def right_copy(s, r):
+    def right_copy(s, h, r):
         core = c if r == 0 else other
         return pltpu.make_async_remote_copy(
-            src_ref=right_send.at[core],
-            dst_ref=right_recv.at[s, r],
-            send_sem=right_send_sems.at[s, r],
-            recv_sem=right_recv_sems.at[s, r],
+            src_ref=right_send.at[core, h],
+            dst_ref=right_recv.at[s, h, r],
+            send_sem=right_send_sems.at[s, h, r],
+            recv_sem=right_recv_sems.at[s, h, r],
             device_id=core_at(bit_xor(a, s, groups), z, core),
             device_id_type=MESH,
         )
 
-    right_copies = [
-        right_copy(s, r) for n, s in enumerate(turns) for r in range(CORES) if (n, r) != (0, 0)
-    ]
-    for copy in right_copies:
-        copy.start()
-
+    order = [(0, h) for h in range(pieces)]
+    order += [(s, h) for h in range(pieces) for s in range(groups // 2, groups)]
+    order += [(s, h) for h in range(pieces) for s in range(1, groups // 2)]
+
+    right_copies = []
+    for s, h in order:
+        for r in range(CORES):
+            if s > 0 or r > 0:
+                copy = right_copy(s, h, r)
+                copy.start()
+                right_copies.append(copy)
+
+    got_left.wait()
     left = jnp.dot(ready, left_weight[...], preferred_element_type=F32).astype(BF16)
     left_send[...] = left
     left_f[0] = left.astype(F32)
@@ -121,41 +125,42 @@
     )
     left_copy.start()
 
+    got_gate.wait()
     gate[...] = jax.nn.sigmoid(jnp.dot(ready, out_gate[...], preferred_element_type=F32))
 
     left_copy.wait_recv()
     left_f[1] = left_recv[...].astype(F32)
 
     part_copies = []
-    for n, s in enumerate(turns):
-        if n == 0:
-            right_f[0] = right_send[c].astype(F32)
+    for s, h in order:
+        if s == 0:
+            right_f[0] = right_send[c, h].astype(F32)
         else:
-            right_copy(s, 0).wait_recv()
-            right_f[0] = right_recv[s, 0].astype(F32)
-        right_copy(s, 1).wait_recv()
-        right_f[1] = right_recv[s, 1].astype(F32)
+            right_copy(s, h, 0).wait_recv()
+            right_f[0] = right_recv[s, h, 0].astype(F32)
+        right_copy(s, h, 1).wait_recv()
+        right_f[1] = right_recv[s, h, 1].astype(F32)
 
         def step(k, sums):
             sums = list(sums)
             for r in range(CORES):
                 line = left_f[r, pl.ds(pl.multiple_of(k * rows, 8), rows), :]
-                for j in range(half):
-                    sums[j] = sums[j] + line * right_f[r, pl.ds(k * half + j, 1), :]
+                for j in range(some):
+                    sums[j] = sums[j] + line * right_f[r, pl.ds(k * some + j, 1), :]
             return tuple(sums)
 
         sums = lax.fori_loop(
-            0, cols, step, tuple(jnp.zeros((rows, width), F32) for _ in range(half))
+            0, cols, step, tuple(jnp.zeros((rows, width), F32) for _ in range(some))
         )
         part = jnp.concatenate(sums, axis=0)
-        part_send[n] = part.astype(BF16)
+        part_send[s, h] = part.astype(BF16)
         layer = bit_xor(a, s, groups)
         turn = bit_xor(layer, z, groups)
         copy = pltpu.make_async_remote_copy(
-            src_ref=part_send.at[n],
-            dst_ref=part_recv.at[turn],
-            send_sem=part_send_sems.at[n],
-            recv_sem=part_recv_sems.at[turn],
+            src_ref=part_send.at[s, h],
+            dst_ref=part_recv.at[turn, h],
+            send_sem=part_send_sems.at[s, h],
+            recv_sem=part_recv_sems.at[turn, h],
             device_id=core_at(a, layer, c),
             device_id_type=MESH,
         )
@@ -166,26 +171,30 @@
 
         @pl.when(turn == 0)
         def _():
-            own_part[...] = part
+            own_part[h] = part
 
         part_copies.append((turn, copy))
 
-    total = own_part[...]
-    for t in range(1, groups):
-        pltpu.make_async_remote_copy(
-            src_ref=part_send.at[0],
-            dst_ref=part_recv.at[t],
-            send_sem=part_send_sems.at[0],
-            recv_sem=part_recv_sems.at[t],
-            device_id=core_at(a, bit_xor(z, t, groups), c),
-            device_id_type=MESH,
-        ).wait_recv()
-        total = total + part_recv[t].astype(F32)
-
-    mixed = (total * count ** (-0.5)).astype(BF16).astype(F32)
-    scaled = unit_channels(mixed, mid_gain[...].reshape(1, width)).astype(BF16)
-    result = jnp.dot(scaled, out_weight[...], preferred_element_type=F32) * gate[...]
-    out_ref[...] = result.reshape(cols, rows, width).astype(BF16)
+    got_mid_gain.wait()
+    got_out.wait()
+    for h in range(pieces):
+        total = own_part[h]
+        for t in range(1, groups):
+            pltpu.make_async_remote_copy(
+                src_ref=part_send.at[0, h],
+                dst_ref=part_recv.at[t, h],
+                send_sem=part_send_sems.at[0, h],
+                recv_sem=part_recv_sems.at[t, h],
+                device_id=core_at(a, bit_xor(z, t, groups), c),
+                device_id_type=MESH,
+            ).wait_recv()
+            total = total + part_recv[t, h].astype(F32)
+
+        mixed = (total * count ** (-0.5)).astype(BF16).astype(F32)
+        scaled = unit_channels(mixed, mid_gain[...].reshape(1, width)).astype(BF16)
+        result = jnp.dot(scaled, out_weight[...], preferred_element_type=F32)
+        result = result * gate[h * some * rows : (h + 1) * some * rows, :]
+        out_ref[h * some : (h + 1) * some] = result.reshape(some, rows, width).astype(BF16)
 
     left_copy.wait_send()
     for copy in right_copies:
@@ -202,9 +211,10 @@
     groups = lax.axis_size("first")
     count = cols * lax.axis_size("second")
     pairs = rows * cols
-    half = pairs // CORES
+    pieces = PIECES if rows // CORES % PIECES == 0 else 1
+    some = rows // CORES // pieces
     changed = pl.pallas_call(
-        functools.partial(triangle_kernel, groups, count),
+        functools.partial(triangle_kernel, groups, count, pieces),
         out_shape=jax.ShapeDtypeStruct((cols, rows, width), BF16),
         in_specs=[pl.BlockSpec(memory_space=pltpu.MemorySpace.HBM)] * 7,
         out_specs=pl.BlockSpec(memory_space=pltpu.VMEM),
@@ -219,20 +229,20 @@
             pltpu.SemaphoreType.DMA((7,)),
             pltpu.VMEM((pairs, width), BF16),
             pltpu.VMEM((pairs, width), BF16),
-            pltpu.VMEM((CORES, half, width), BF16),
-            pltpu.VMEM((groups, CORES, half, width), BF16),
+            pltpu.VMEM((CORES, pieces, cols * some, width), BF16),
+            pltpu.VMEM((groups, pieces, CORES, cols * some, width), BF16),
             pltpu.VMEM((pairs, width), F32),
             pltpu.VMEM((CORES, pairs, width), F32),
-            pltpu.VMEM((CORES, half, width), F32),
-            pltpu.VMEM((groups, pairs, width), BF16),
-            pltpu.VMEM((groups, pairs, width), BF16),
-            pltpu.VMEM((pairs, width), F32),
+            pltpu.VMEM((CORES, cols * some, width), F32),
+            pltpu.VMEM((groups, pieces, rows * some, width), BF16),
+            pltpu.VMEM((groups, pieces, rows * some, width), BF16),
+            pltpu.VMEM((pieces, rows * some, width), F32),
             pltpu.VMEM((pairs, width), F32),
             pltpu.SemaphoreType.DMA((2,)),
-            pltpu.SemaphoreType.DMA((groups, CORES)),
-            pltpu.SemaphoreType.DMA((groups, CORES)),
-            pltpu.SemaphoreType.DMA((groups,)),
-            pltpu.SemaphoreType.DMA((groups,)),
+            pltpu.SemaphoreType.DMA((groups, pieces, CORES)),
+            pltpu.SemaphoreType.DMA((groups, pieces, CORES)),
+            pltpu.SemaphoreType.DMA((groups, pieces)),
+            pltpu.SemaphoreType.DMA((groups, pieces)),
         ],
         compiler_params=pltpu.CompilerParams(
             collective_id=0, has_side_effects=True, vmem_limit_bytes=8 * 1024 * 1024

time: 17.7 us -> 17.4 us (0.983)
  the two profiles are of different devices: /device:TPU:13 before, /device:TPU:5 now
where the time goes in v4:
time: 17.4 us; the launch traced here: 17.2 us
  Pallas kernels  16.6 us (95%)
  local copies, waits for them, and re-layouts  0.64 us (4%)
    pallas_call x1, Pallas kernels, by_kernel(): pl.pallas_call(functools.partial(triangle_kernel, groups, count, pieces),...  16.6 us
    unnamed x1, local copies, waits for them, and re-layouts  0.64 us

profile of v4, /device:TPU:5, one launch (start us, length us, event | category | flops | bytes accessed | tf_op | source)
XLA Modules:
  0.0 17.2 jit_solution(9807583613995572538)
XLA Ops:
  0.0 16.6 %shard_map.73 = bf16[12,24,128]{2,1,0:T(8,128)(2,1)S(1)} custom-call(bf16[12,24,128]{2,1,0:T(8,128)(2,1)} %bitcast.3, f32[128]{0:T(128)} %in_gain_hbm.1, bf16[128,128]{1,0:T(8,128)(2,1)} %left_weight_hbm.1, bf16[128,128]{1,0:T(8,128)(2,1)} %right_weight_hbm.1, f32[128]{0:T(128)} %mid_gain_hbm.1, bf16[128,128]{1,0:T(8,128)(2,1)} %out_weight_hbm.1, ...), custom_call_target="tpu_custom_call" | custom-call | tf_op jit(solution)/shard_map/pallas_call | solution.py:216
  16.6 0.6 %copy.9 = bf16[24,12,128]{2,0,1:T(8,128)(2,1)} copy(bf16[24,12,128]{2,0,1:T(8,128)(2,1)S(1)} %bitcast.2) | data formatting | bytes 147456

commit v5 on v4

--- a/solution.py
+++ b/solution.py
@@ -38,7 +38,7 @@
     x_ref, in_gain, left_weight, right_weight, mid_gain, out_weight, out_gate, fetch_sems,
     left_send, left_recv, right_send, right_recv, right_rows, left_f, right_f,
     part_send, part_recv, own_part, gate,
-    left_sems, right_send_sems, right_recv_sems, part_send_sems, part_recv_sems,
+    line_sems, left_sems, right_send_sems, right_recv_sems, part_send_sems, part_recv_sems,
 ):
     cols, rows, width = x_ref.shape
     half = rows // CORES
@@ -56,9 +56,20 @@
     peers = [core_at(a, z, other)]
     for s in range(1, groups):
         peers += [core_at(bit_xor(a, s, groups), z, c), core_at(bit_xor(a, s, groups), z, other)]
-        peers.append(core_at(a, bit_xor(z, s, groups), c))
     for peer in peers:
         pl.semaphore_signal(barrier, inc=1, device_id=peer, device_id_type=MESH)
+
+    def greet_line(semaphore):
+        for there, near in ((z > 0, z - 1), (z < groups - 1, z + 1)):
+
+            @pl.when(there)
+            def _(near=near):
+                pl.semaphore_signal(
+                    semaphore, inc=1, device_id=core_at(a, near, c), device_id_type=MESH
+                )
+
+    neighbours = (z + groups - 1) // groups + (2 * groups - 2 - z) // groups
+    greet_line(barrier)
 
     fetches = [
         pltpu.make_async_copy(src, dst, fetch_sems.at[n])
@@ -86,7 +97,8 @@
                 right_f[p, k * some : (k + 1) * some, :] = right_rows[start : start + some, :]
             right_send[p, h] = right_f[p].astype(BF16)
 
-    pl.semaphore_wait(barrier, len(peers))
+    pl.semaphore_wait(barrier, len(peers) + neighbours)
+    greet_line(line_sems.at[0])
 
     def right_copy(s, h, r):
         core = c if r == 0 else other
@@ -127,6 +139,11 @@
 
     got_gate.wait()
     gate[...] = jax.nn.sigmoid(jnp.dot(ready, out_gate[...], preferred_element_type=F32))
+
+    for n in range(groups - 2):
+        pl.semaphore_wait(line_sems.at[n], neighbours)
+        if n + 1 < groups - 2:
+            greet_line(line_sems.at[n + 1])
 
     left_copy.wait_recv()
     left_f[1] = left_recv[...].astype(F32)
@@ -238,6 +255,7 @@
             pltpu.VMEM((groups, pieces, rows * some, width), BF16),
             pltpu.VMEM((pieces, rows * some, width), F32),
             pltpu.VMEM((pairs, width), F32),
+            pltpu.SemaphoreType.REGULAR((groups - 2,)),
             pltpu.SemaphoreType.DMA((2,)),
             pltpu.SemaphoreType.DMA((groups, pieces, CORES)),
             pltpu.SemaphoreType.DMA((groups, pieces, CORES)),
@@ -300,7 +318,7 @@
     rows, cols, width = pair_state.shape
     fits = (
         parts == CORES * groups
-        and groups > 1
+        and groups > 2
         and groups & (groups - 1) == 0
         and rows == CORES * cols
         and rows % 8 == 0

time: 17.4 us -> 17.4 us (level)
  no operation moved by 1% of the time
where the time goes in v5:
time: 17.4 us; the launch traced here: 17.2 us
  Pallas kernels  16.6 us (95%)
  local copies, waits for them, and re-layouts  0.64 us (4%)
    pallas_call x1, Pallas kernels, by_kernel(): pl.pallas_call(functools.partial(triangle_kernel, groups, count, pieces),...  16.6 us
    unnamed x1, local copies, waits for them, and re-layouts  0.64 us

profile of v5, /device:TPU:5, one launch (start us, length us, event | category | flops | bytes accessed | tf_op | source)
XLA Modules:
  0.0 17.2 jit_solution(9122308097896669240)
XLA Ops:
  0.0 16.6 %shard_map.73 = bf16[12,24,128]{2,1,0:T(8,128)(2,1)S(1)} custom-call(bf16[12,24,128]{2,1,0:T(8,128)(2,1)} %bitcast.3, f32[128]{0:T(128)} %in_gain_hbm.1, bf16[128,128]{1,0:T(8,128)(2,1)} %left_weight_hbm.1, bf16[128,128]{1,0:T(8,128)(2,1)} %right_weight_hbm.1, f32[128]{0:T(128)} %mid_gain_hbm.1, bf16[128,128]{1,0:T(8,128)(2,1)} %out_weight_hbm.1, ...), custom_call_target="tpu_custom_call" | custom-call | tf_op jit(solution)/shard_map/pallas_call | solution.py:233
  16.6 0.6 %copy.9 = bf16[24,12,128]{2,0,1:T(8,128)(2,1)} copy(bf16[24,12,128]{2,0,1:T(8,128)(2,1)S(1)} %bitcast.2) | data formatting | bytes 147456

commit v6 on v5

--- a/solution.py
+++ b/solution.py
@@ -111,9 +111,8 @@
             device_id_type=MESH,
         )
 
-    order = [(0, h) for h in range(pieces)]
-    order += [(s, h) for h in range(pieces) for s in range(groups // 2, groups)]
-    order += [(s, h) for h in range(pieces) for s in range(1, groups // 2)]
+    order = [(s, h) for s in (0, groups - 1) for h in range(pieces)]
+    order += [(s, h) for h in range(pieces) for s in range(groups - 2, 0, -1)]
 
     right_copies = []
     for s, h in order:

time: 17.4 us -> 17 us (0.977)
  Pallas kernels: 16.6 us -> 16.2 us
    pallas_call x1, Pallas kernels: 16.6 us -> 16.2 us  [by_kernel(): pl.pallas_call(functools.partial(triangle_kernel, groups, count, pieces),...]
where the time goes in v6:
time: 17 us; the launch traced here: 16.8 us
  Pallas kernels  16.2 us (95%)
  local copies, waits for them, and re-layouts  0.64 us (4%)
    pallas_call x1, Pallas kernels, by_kernel(): pl.pallas_call(functools.partial(triangle_kernel, groups, count, pieces),...  16.2 us
    unnamed x1, local copies, waits for them, and re-layouts  0.64 us

profile of v6, /device:TPU:5, one launch (start us, length us, event | category | flops | bytes accessed | tf_op | source)
XLA Modules:
  0.0 16.8 jit_solution(9219059633329046869)
XLA Ops:
  0.0 16.2 %shard_map.73 = bf16[12,24,128]{2,1,0:T(8,128)(2,1)S(1)} custom-call(bf16[12,24,128]{2,1,0:T(8,128)(2,1)} %bitcast.3, f32[128]{0:T(128)} %in_gain_hbm.1, bf16[128,128]{1,0:T(8,128)(2,1)} %left_weight_hbm.1, bf16[128,128]{1,0:T(8,128)(2,1)} %right_weight_hbm.1, f32[128]{0:T(128)} %mid_gain_hbm.1, bf16[128,128]{1,0:T(8,128)(2,1)} %out_weight_hbm.1, ...), custom_call_target="tpu_custom_call" | custom-call | tf_op jit(solution)/shard_map/pallas_call | solution.py:232
  16.2 0.6 %copy.9 = bf16[24,12,128]{2,0,1:T(8,128)(2,1)} copy(bf16[24,12,128]{2,0,1:T(8,128)(2,1)S(1)} %bitcast.2) | data formatting | bytes 147456

commit v7 on v4

--- a/solution.py
+++ b/solution.py
@@ -99,9 +99,8 @@
             device_id_type=MESH,
         )
 
-    order = [(0, h) for h in range(pieces)]
-    order += [(s, h) for h in range(pieces) for s in range(groups // 2, groups)]
-    order += [(s, h) for h in range(pieces) for s in range(1, groups // 2)]
+    order = [(s, h) for s in (0, groups - 1) for h in range(pieces)]
+    order += [(s, h) for h in range(pieces) for s in range(groups - 2, 0, -1)]
 
     right_copies = []
     for s, h in order:

time: 17.4 us -> 16.9 us (0.971)
  Pallas kernels: 16.6 us -> 16.1 us
    pallas_call x1, Pallas kernels: 16.6 us -> 16.1 us  [by_kernel(): pl.pallas_call(functools.partial(triangle_kernel, groups, count, pieces),...]
where the time goes in v7:
time: 16.9 us; the launch traced here: 16.8 us
  Pallas kernels  16.1 us (95%)
  local copies, waits for them, and re-layouts  0.64 us (4%)
    pallas_call x1, Pallas kernels, by_kernel(): pl.pallas_call(functools.partial(triangle_kernel, groups, count, pieces),...  16.1 us
    unnamed x1, local copies, waits for them, and re-layouts  0.64 us

profile of v7, /device:TPU:5, one launch (start us, length us, event | category | flops | bytes accessed | tf_op | source)
XLA Modules:
  0.0 16.8 jit_solution(8109638474201109572)
XLA Ops:
  0.0 16.1 %shard_map.73 = bf16[12,24,128]{2,1,0:T(8,128)(2,1)S(1)} custom-call(bf16[12,24,128]{2,1,0:T(8,128)(2,1)} %bitcast.3, f32[128]{0:T(128)} %in_gain_hbm.1, bf16[128,128]{1,0:T(8,128)(2,1)} %left_weight_hbm.1, bf16[128,128]{1,0:T(8,128)(2,1)} %right_weight_hbm.1, f32[128]{0:T(128)} %mid_gain_hbm.1, bf16[128,128]{1,0:T(8,128)(2,1)} %out_weight_hbm.1, ...), custom_call_target="tpu_custom_call" | custom-call | tf_op jit(solution)/shard_map/pallas_call | solution.py:215
  16.1 0.6 %copy.9 = bf16[24,12,128]{2,0,1:T(8,128)(2,1)} copy(bf16[24,12,128]{2,0,1:T(8,128)(2,1)S(1)} %bitcast.2) | data formatting | bytes 147456

commit v8 on v7

--- a/solution.py
+++ b/solution.py
@@ -124,9 +124,6 @@
     )
     left_copy.start()
 
-    got_gate.wait()
-    gate[...] = jax.nn.sigmoid(jnp.dot(ready, out_gate[...], preferred_element_type=F32))
-
     left_copy.wait_recv()
     left_f[1] = left_recv[...].astype(F32)
 
@@ -174,6 +171,8 @@
 
         part_copies.append((turn, copy))
 
+    got_gate.wait()
+    gate[...] = jax.nn.sigmoid(jnp.dot(ready, out_gate[...], preferred_element_type=F32))
     got_mid_gain.wait()
     got_out.wait()
     for h in range(pieces):

time: 16.9 us -> 16.9 us (level)
  no operation moved by 1% of the time
where the time goes in v8:
time: 16.9 us; the launch traced here: 16.8 us
  Pallas kernels  16.1 us (95%)
  local copies, waits for them, and re-layouts  0.64 us (4%)
    pallas_call x1, Pallas kernels, by_kernel(): pl.pallas_call(functools.partial(triangle_kernel, groups, count, pieces),...  16.1 us
    unnamed x1, local copies, waits for them, and re-layouts  0.64 us

profile of v8, /device:TPU:5, one launch (start us, length us, event | category | flops | bytes accessed | tf_op | source)
XLA Modules:
  0.0 16.8 jit_solution(250893321424744830)
XLA Ops:
  0.0 16.1 %shard_map.73 = bf16[12,24,128]{2,1,0:T(8,128)(2,1)S(1)} custom-call(bf16[12,24,128]{2,1,0:T(8,128)(2,1)} %bitcast.3, f32[128]{0:T(128)} %in_gain_hbm.1, bf16[128,128]{1,0:T(8,128)(2,1)} %left_weight_hbm.1, bf16[128,128]{1,0:T(8,128)(2,1)} %right_weight_hbm.1, f32[128]{0:T(128)} %mid_gain_hbm.1, bf16[128,128]{1,0:T(8,128)(2,1)} %out_weight_hbm.1, ...), custom_call_target="tpu_custom_call" | custom-call | tf_op jit(solution)/shard_map/pallas_call | solution.py:214
  16.1 0.6 %copy.9 = bf16[24,12,128]{2,0,1:T(8,128)(2,1)} copy(bf16[24,12,128]{2,0,1:T(8,128)(2,1)S(1)} %bitcast.2) | data formatting | bytes 147456
